TPU v7x, 32 devices: a whole 2x2x4 slice. The times are simulated.
32 devices in a mesh: mod: 4 (over y, x), seq: 8 (over z, core).
Axes of the slice: x: 2, y: 2, z: 4, core: 2. Of those that a mesh axis runs over, the one named last changes fastest.
Arguments:
- tokens: bfloat16 [2048, 4096], P(('mod', 'seq')), may hold values from -6 to 6
- norm_gain: float32 [3, 4096], replicated, may hold values from 0.2 to 2.6
- qkv_weight: bfloat16 [3, 4096, 12288], P(None, None, 'seq'), may hold values from -0.45 to 0.45
- out_weight: bfloat16 [3, 4096, 4096], P(None, 'seq'), may hold values from -0.375 to 0.375
- modality: int32 [16], replicated, may hold values from 0 to 2
- doc_lengths: int32 [4], replicated, may hold values from 1 to 1024, 2048 in all
Outputs:
- mixed: bfloat16 [2048, 4096], P(('mod', 'seq'))
Inputs may be any that keep to these rules, and one draw needn't show every extreme that they name: `doc_lengths`: the lengths sum to 2048; documents follow one another from position 0 in the given order.
All inputs are finite; a program needn't handle non-finite values.
Results may differ from a plain program's by a relative error of at most 0.015.
Values may be sent and summed in bfloat16 or wider, within the bound.
A program may use at most 128 MiB of HBM per device.

v0:
```python
import math

import jax
import jax.numpy as jnp
from jax import lax
from jax.sharding import PartitionSpec as P

HDIM = 128
BLOCK = 128


def modes_of_rows(first_row, row_count, modality):
    block_ids = (first_row + jnp.arange(row_count, dtype=jnp.int32)) // BLOCK
    block_table = jnp.arange(modality.shape[0], dtype=jnp.int32)
    picked = jnp.where(block_ids[:, None] == block_table[None, :], modality[None, :], 0)
    return jnp.sum(picked, axis=1)


def documents(positions, doc_lengths):
    doc_ends = jnp.cumsum(doc_lengths)
    return jnp.sum((positions[:, None] >= doc_ends[None, :]).astype(jnp.int32), axis=1)


def body(tokens, norm_gain, qkv_weight, out_weight, modality, doc_lengths):
    row_count = tokens.shape[0]
    seq_count = lax.axis_size("seq")
    mod_count = lax.axis_size("mod")
    group_rows = row_count * seq_count
    mod_index = lax.axis_index("mod")
    own_first = (mod_index * seq_count + lax.axis_index("seq")) * row_count
    row_modes = modes_of_rows(own_first, row_count, modality)
    choose = (
        row_modes[:, None, None] == jnp.arange(norm_gain.shape[0], dtype=jnp.int32)[None, :, None]
    )
    gain_rows = jnp.sum(jnp.where(choose, norm_gain[None, :, :], 0.0), axis=1)
    values = tokens.astype(jnp.float32)
    mean_square = jnp.mean(values * values, axis=1, keepdims=True)
    normed = (values * lax.rsqrt(mean_square + 1e-05) * gain_rows).astype(jnp.bfloat16)
    gathered = lax.all_gather(normed, "seq", axis=0, tiled=True)
    group_first = mod_index * group_rows
    block_count = group_rows // BLOCK
    block_modes = lax.dynamic_slice_in_dim(modality, group_first // BLOCK, block_count)
    heads_here = qkv_weight.shape[2] // (3 * HDIM)

    def project(block_pair):
        row_block, block_mode = block_pair
        weight = lax.dynamic_index_in_dim(qkv_weight, block_mode, 0, keepdims=False)
        return jnp.dot(row_block, weight, preferred_element_type=jnp.float32).astype(jnp.bfloat16)

    projected = lax.map(
        project, (gathered.reshape(block_count, BLOCK, gathered.shape[1]), block_modes)
    )
    projected = projected.reshape(group_rows, heads_here, 3, HDIM)
    queries = projected[:, :, 0, :]
    keys_here = projected[:, :, 1, :]
    values_here = projected[:, :, 2, :]
    quarter = group_rows // mod_count
    local_rows = jnp.arange(group_rows, dtype=jnp.int32)
    query_pos = group_first + local_rows
    query_docs = documents(query_pos, doc_lengths)
    block_size = min(512, quarter)
    block_total = group_rows // block_size
    score_scale = 1.0 / math.sqrt(HDIM)
    query_blocks = queries.reshape(block_total, block_size, heads_here, HDIM)
    pos_blocks = query_pos.reshape(block_total, block_size)
    doc_blocks = query_docs.reshape(block_total, block_size)
    start_state = (
        jnp.full((block_total, heads_here, block_size), -1e30, jnp.float32),
        jnp.zeros((block_total, heads_here, block_size), jnp.float32),
        jnp.zeros((block_total, block_size, heads_here, HDIM), jnp.float32),
    )
    key_start = jnp.int32(0)
    piece_keys = lax.all_gather(keys_here, "mod", axis=0, tiled=True)
    piece_values = lax.all_gather(values_here, "mod", axis=0, tiled=True)
    key_count = piece_keys.shape[0]
    key_pos = jnp.arange(key_count, dtype=jnp.int32)
    key_docs = documents(key_pos, doc_lengths)

    def one_block(block_state):
        row_max, totals, summed_rows, query_block, block_pos, block_docs = block_state

        def attend(unused):
            scores = (
                jnp.einsum(
                    "qhc,khc->hqk", query_block, piece_keys, preferred_element_type=jnp.float32
                )
                * score_scale
            )
            allowed = (
                (key_pos[None, :] <= block_pos[:, None])
                & (key_docs[None, :] == block_docs[:, None])
            )[None, :, :]
            new_max = jnp.maximum(row_max, jnp.max(jnp.where(allowed, scores, -1e30), axis=2))
            weights = jnp.where(allowed, jnp.exp(scores - new_max[:, :, None]), 0.0)
            rescale = jnp.exp(row_max - new_max)
            new_totals = totals * rescale + jnp.sum(weights, axis=2)
            added_rows = jnp.einsum(
                "hqk,khc->qhc",
                weights.astype(jnp.bfloat16),
                piece_values,
                preferred_element_type=jnp.float32,
            )
            new_rows = summed_rows * jnp.transpose(rescale)[:, :, None] + added_rows
            return (new_max, new_totals, new_rows)

        def keep_state(unused):
            return (row_max, totals, summed_rows)

        return lax.cond(key_start <= jnp.max(block_pos), attend, keep_state, 0)

    row_max, totals, summed_rows = lax.map(
        one_block,
        (start_state[0], start_state[1], start_state[2], query_blocks, pos_blocks, doc_blocks),
    )
    divisor = jnp.transpose(totals, (0, 2, 1))[:, :, :, None]
    attended = (summed_rows / divisor).astype(jnp.bfloat16).reshape(group_rows, heads_here * HDIM)

    def output(block_pair):
        row_block, block_mode = block_pair
        weight = lax.dynamic_index_in_dim(out_weight, block_mode, 0, keepdims=False)
        return jnp.dot(row_block, weight, preferred_element_type=jnp.float32)

    partial_value = lax.map(
        output, (attended.reshape(block_count, BLOCK, attended.shape[1]), block_modes)
    )
    head_sums = lax.psum_scatter(
        partial_value.reshape(group_rows, partial_value.shape[2]).astype(jnp.bfloat16),
        "seq",
        scatter_dimension=0,
        tiled=True,
    ).astype(jnp.float32)
    return (tokens.astype(jnp.float32) + head_sums).astype(jnp.bfloat16)


def solution(mesh):
    return jax.shard_map(
        body,
        mesh=mesh,
        in_specs=(
            P(("mod", "seq"), None),
            P(),
            P(None, None, "seq"),
            P(None, "seq", None),
            P(),
            P(),
        ),
        out_specs=P(("mod", "seq"), None),
        check_vma=False,
    )
```

profile of v0, /device:TPU:13, one launch (start us, length us, event | category | flops | bytes accessed | tf_op | source)
XLA Modules:
  0.0 283.4 jit_solution(8059738032792153300)
XLA Ops:
  9.9 2.0 fusion.50
  12.2 47.1 %all-gather.6.cloned.1.call-done = bf16[512,4096]{1,0:T(8,128)(2,1)} async-done(((bf16[64,4096]{1,0:T(8,128)(2,1)}), bf16[512,4096]{1,0:T(8,128)(2,1)}) %all-gather.6.cloned.1.call-update) | async-done | bytes 4194320 | tf_op jit(solution)/shard_map/all_gather | solution.py:39
  59.3 37.1 %while.33 = (s32[]{:T(128)}, bf16[4,128,1536]{2,1,0:T(8,128)(2,1)S(1)}, bf16[4,128,4096]{2,1,0:T(8,128)(2,1)}, s32[4]{0:T(128)S(1)}, bf16[3,4096,1536]{2,1,0:T(8,128)(2,1)}, /*index=5*/s32[]{:T(128)}, s32[]{:T(128)}, s32[]{:T(128)}) while((s32[]{:T(128)}, bf16[4,128,1536]{2,1,0:T(8,128)(2,1)S(1)}, bf16[4,128,4096]{2,1,0:T(8,128)(2,1)}, ...), condition=%wide.region_4.5_spmd, body=%wide.region_3.4_spmd.sunk | while | flops 1610809344 | bytes 14025863 | solution.py:50
  61.8 6.7 %fusion.65 = bf16[4,128,1536]{2,1,0:T(8,128)(2,1)S(1)} fusion(bf16[4,128,1536]{2,1,0:T(8,128)(2,1)S(1)} %get-tuple-element.457, s32[]{:T(128)} %get-tuple-element.456, bf16[3,4096,1536]{2,1,0:T(8,128)(2,1)} %get-tuple-element.468, s32[]{:T(128)S(6)} %select_n.67, bf16[4,128,4096]{2,1,0:T(8,128)(2,1)} %get-tuple-element.466), kind=kOutput, calls=%fused_computation.6.clone.1 | convolution fusion | flops 1610809344 | bytes 14025732 | tf_op jit(solution)/shard_map/while/body/eval_jaxpr/dot_general | solution.py:48
  71.1 6.7 %fusion.65 = bf16[4,128,1536]{2,1,0:T(8,128)(2,1)S(1)} fusion(bf16[4,128,1536]{2,1,0:T(8,128)(2,1)S(1)} %get-tuple-element.457, s32[]{:T(128)} %get-tuple-element.456, bf16[3,4096,1536]{2,1,0:T(8,128)(2,1)} %get-tuple-element.468, s32[]{:T(128)S(6)} %select_n.67, bf16[4,128,4096]{2,1,0:T(8,128)(2,1)} %get-tuple-element.466), kind=kOutput, calls=%fused_computation.6.clone.1 | convolution fusion | flops 1610809344 | bytes 14025732 | tf_op jit(solution)/shard_map/while/body/eval_jaxpr/dot_general | solution.py:48
  80.4 6.7 %fusion.65 = bf16[4,128,1536]{2,1,0:T(8,128)(2,1)S(1)} fusion(bf16[4,128,1536]{2,1,0:T(8,128)(2,1)S(1)} %get-tuple-element.457, s32[]{:T(128)} %get-tuple-element.456, bf16[3,4096,1536]{2,1,0:T(8,128)(2,1)} %get-tuple-element.468, s32[]{:T(128)S(6)} %select_n.67, bf16[4,128,4096]{2,1,0:T(8,128)(2,1)} %get-tuple-element.466), kind=kOutput, calls=%fused_computation.6.clone.1 | convolution fusion | flops 1610809344 | bytes 14025732 | tf_op jit(solution)/shard_map/while/body/eval_jaxpr/dot_general | solution.py:48
  89.6 6.7 %fusion.65 = bf16[4,128,1536]{2,1,0:T(8,128)(2,1)S(1)} fusion(bf16[4,128,1536]{2,1,0:T(8,128)(2,1)S(1)} %get-tuple-element.457, s32[]{:T(128)} %get-tuple-element.456, bf16[3,4096,1536]{2,1,0:T(8,128)(2,1)} %get-tuple-element.468, s32[]{:T(128)S(6)} %select_n.67, bf16[4,128,4096]{2,1,0:T(8,128)(2,1)} %get-tuple-element.466), kind=kOutput, calls=%fused_computation.6.clone.1 | convolution fusion | flops 1610809344 | bytes 14025732 | tf_op jit(solution)/shard_map/while/body/eval_jaxpr/dot_general | solution.py:48
  100.8 33.1 %all-gather.8.cloned.1.call-done = bf16[2048,4,1,128]{0,3,2,1:T(8,128)(2,1)} async-done(((bf16[512,4,1,128]{0,3,2,1:T(8,128)(2,1)}), bf16[2048,4,1,128]{0,3,2,1:T(8,128)(2,1)}) %all-gather.8.cloned.1.call-update) | async-done | bytes 2097168 | tf_op jit(solution)/shard_map/all_gather | solution.py:73
  134.0 3.0 %copy.17 = bf16[2048,4,128]{2,0,1:T(8,128)(2,1)S(1)} copy(bf16[2048,4,128]{0,2,1:T(8,128)(2,1)} %bitcast.85) | data formatting | bytes 4194304
  137.0 33.9 %all-gather.10.cloned.1.call-done = bf16[2048,4,1,128]{0,3,2,1:T(8,128)(2,1)} async-done(((bf16[512,4,1,128]{0,3,2,1:T(8,128)(2,1)}), bf16[2048,4,1,128]{0,3,2,1:T(8,128)(2,1)}) %all-gather.10.cloned.1.call-update) | async-done | bytes 2097168 | tf_op jit(solution)/shard_map/all_gather | solution.py:74
  170.9 4.0 %copy.18 = bf16[2048,4,128]{2,0,1:T(8,128)(2,1)} copy(bf16[2048,4,128]{0,2,1:T(8,128)(2,1)} %bitcast.86) | data formatting | bytes 4194304
  174.8 23.8 %while.35 = (s32[]{:T(128)}, f32[4,4,128]{2,1,0:T(4,128)S(1)}, f32[4,128,4,128]{1,3,2,0:T(8,128)}, s32[4,128]{1,0:T(4,128)S(1)}, s32[2048]{0:T(1024)S(1)}, /*ind...) while((s32[]{:T(128)}, f32[4,4,128]{2,1,0:T(4,128)S(1)}, ...), condition=%wide.region_14.15_spmd.clone, body=%wide.region_8.14_spmd.clone.sunk | while | flops 549324416 | bytes 28503860 | solution.py:111
  176.2 3.7 %conditional.3 = (f32[1,4,128]{2,1,0:T(4,128)S(1)}, f32[1,128,4,128]{3,1,2,0:T(8,128)S(1)}) conditional(s32[]{:T(128)} %convert_element_type.82, (f32[4,128]{1,0:T(4,128)S(1)}, f32[128,4,128]{2,0,1:T(8,128)S(1)}) %tuple.105, (s32[2048]{0:T(1024)S(1)}, s32[1,128]{1,0:T(1,128)S(1)}, s32[2048]{0:T(1024)S(1)}, s32[4,128]{1,0:T(4,128)S(1)}, s32[]{:T(128)}, ...), branch_computations={%region_10.10_spmd, %region_11.13_spmd} | conditional | flops 549324288 | bytes 26912820 | solution.py:109
  182.1 3.7 %conditional.3 = (f32[1,4,128]{2,1,0:T(4,128)S(1)}, f32[1,128,4,128]{3,1,2,0:T(8,128)S(1)}) conditional(s32[]{:T(128)} %convert_element_type.82, (f32[4,128]{1,0:T(4,128)S(1)}, f32[128,4,128]{2,0,1:T(8,128)S(1)}) %tuple.105, (s32[2048]{0:T(1024)S(1)}, s32[1,128]{1,0:T(1,128)S(1)}, s32[2048]{0:T(1024)S(1)}, s32[4,128]{1,0:T(4,128)S(1)}, s32[]{:T(128)}, ...), branch_computations={%region_10.10_spmd, %region_11.13_spmd} | conditional | flops 549324288 | bytes 26912820 | solution.py:109
  188.0 3.7 %conditional.3 = (f32[1,4,128]{2,1,0:T(4,128)S(1)}, f32[1,128,4,128]{3,1,2,0:T(8,128)S(1)}) conditional(s32[]{:T(128)} %convert_element_type.82, (f32[4,128]{1,0:T(4,128)S(1)}, f32[128,4,128]{2,0,1:T(8,128)S(1)}) %tuple.105, (s32[2048]{0:T(1024)S(1)}, s32[1,128]{1,0:T(1,128)S(1)}, s32[2048]{0:T(1024)S(1)}, s32[4,128]{1,0:T(4,128)S(1)}, s32[]{:T(128)}, ...), branch_computations={%region_10.10_spmd, %region_11.13_spmd} | conditional | flops 549324288 | bytes 26912820 | solution.py:109
  194.0 3.7 %conditional.3 = (f32[1,4,128]{2,1,0:T(4,128)S(1)}, f32[1,128,4,128]{3,1,2,0:T(8,128)S(1)}) conditional(s32[]{:T(128)} %convert_element_type.82, (f32[4,128]{1,0:T(4,128)S(1)}, f32[128,4,128]{2,0,1:T(8,128)S(1)}) %tuple.105, (s32[2048]{0:T(1024)S(1)}, s32[1,128]{1,0:T(1,128)S(1)}, s32[2048]{0:T(1024)S(1)}, s32[4,128]{1,0:T(4,128)S(1)}, s32[]{:T(128)}, ...), branch_computations={%region_10.10_spmd, %region_11.13_spmd} | conditional | flops 549324288 | bytes 26912820 | solution.py:109
  198.6 1.3 divide_convert_fusion
  200.0 25.9 %while.34 = (s32[]{:T(128)}, bf16[4,128,4096]{2,1,0:T(8,128)(2,1)}, bf16[4,128,512]{1,2,0:T(8,128)(2,1)S(1)}, s32[4]{0:T(128)S(1)}, bf16[3,512,4096]{2,1,0:T(8,128)(2,1)}, /*index=5*/s32[]{:T(128)}, s32[]{:T(128)}, s32[]{:T(128)}) while((s32[]{:T(128)}, bf16[4,128,4096]{2,1,0:T(8,128)(2,1)}, bf16[4,128,512]{1,2,0:T(8,128)(2,1)S(1)}, ...), condition=%wide.region_16.17_spmd, body=%wide.region_15.16_spmd.sunk | while | flops 536870912 | bytes 6423687 | solution.py:123
  202.5 3.9 %fusion.68 = bf16[4,128,4096]{2,1,0:T(8,128)(2,1)} fusion(bf16[4,128,4096]{2,1,0:T(8,128)(2,1)} %get-tuple-element.517, s32[]{:T(128)} %get-tuple-element.516, bf16[3,512,4096]{2,1,0:T(8,128)(2,1)} %get-tuple-element.528, s32[]{:T(128)S(6)} %select_n.68, bf16[4,128,512]{1,2,0:T(8,128)(2,1)S(1)} %get-tuple-element.526), kind=kOutput, calls=%fused_computation.36.clone.1 | convolution fusion | flops 536870912 | bytes 6423556 | tf_op jit(solution)/shard_map/while/body/eval_jaxpr/dot_general | solution.py:121
  209.0 4.0 %fusion.68 = bf16[4,128,4096]{2,1,0:T(8,128)(2,1)} fusion(bf16[4,128,4096]{2,1,0:T(8,128)(2,1)} %get-tuple-element.517, s32[]{:T(128)} %get-tuple-element.516, bf16[3,512,4096]{2,1,0:T(8,128)(2,1)} %get-tuple-element.528, s32[]{:T(128)S(6)} %select_n.68, bf16[4,128,512]{1,2,0:T(8,128)(2,1)S(1)} %get-tuple-element.526), kind=kOutput, calls=%fused_computation.36.clone.1 | convolution fusion | flops 536870912 | bytes 6423556 | tf_op jit(solution)/shard_map/while/body/eval_jaxpr/dot_general | solution.py:121
  215.5 3.9 %fusion.68 = bf16[4,128,4096]{2,1,0:T(8,128)(2,1)} fusion(bf16[4,128,4096]{2,1,0:T(8,128)(2,1)} %get-tuple-element.517, s32[]{:T(128)} %get-tuple-element.516, bf16[3,512,4096]{2,1,0:T(8,128)(2,1)} %get-tuple-element.528, s32[]{:T(128)S(6)} %select_n.68, bf16[4,128,512]{1,2,0:T(8,128)(2,1)S(1)} %get-tuple-element.526), kind=kOutput, calls=%fused_computation.36.clone.1 | convolution fusion | flops 536870912 | bytes 6423556 | tf_op jit(solution)/shard_map/while/body/eval_jaxpr/dot_general | solution.py:121
  221.9 3.9 %fusion.68 = bf16[4,128,4096]{2,1,0:T(8,128)(2,1)} fusion(bf16[4,128,4096]{2,1,0:T(8,128)(2,1)} %get-tuple-element.517, s32[]{:T(128)} %get-tuple-element.516, bf16[3,512,4096]{2,1,0:T(8,128)(2,1)} %get-tuple-element.528, s32[]{:T(128)S(6)} %select_n.68, bf16[4,128,512]{1,2,0:T(8,128)(2,1)S(1)} %get-tuple-element.526), kind=kOutput, calls=%fused_computation.36.clone.1 | convolution fusion | flops 536870912 | bytes 6423556 | tf_op jit(solution)/shard_map/while/body/eval_jaxpr/dot_general | solution.py:121
  225.9 49.0 %reduce-scatter.2.cloned.1.call-done = bf16[64,4096]{1,0:T(8,128)(2,1)} async-done(((bf16[512,4096]{1,0:T(8,128)(2,1)}), bf16[64,4096]{1,0:T(8,128)(2,1)}) %reduce-scatter.2.cloned.1.call-update) | async-done | bytes 524304 | tf_op jit(solution)/shard_map/reduce_scatter | solution.py:126
  274.9 2.0 fusion.51
  (115 shorter events, 33.3 us)
Async XLA Ops:
  6.5 5.5 %copy-start.2 = (s32[16]{0:T(128)S(1)}, s32[16]{0:T(128)}, u32[]{:S(2)}) copy-start(s32[16]{0:T(128)} %param.18) | copy-start | bytes 196
  6.5 52.7 %all-gather.6.cloned.1.call-start = ((), (), s32[]{:S(2)}) async-start(), calls=%async_computation.1 | async-start | bytes 4718592 | tf_op jit(solution)/shard_map/all_gather | solution.py:39
  12.0 122.0 %all-gather.8.cloned.1.call-start = ((), (), s32[]{:S(2)}) async-start(), calls=%async_computation.3 | async-start | bytes 2621440 | tf_op jit(solution)/shard_map/all_gather | solution.py:73
  97.5 2.6 copy-start.3
  99.3 71.6 %all-gather.10.cloned.1.call-start = ((), (), s32[]{:S(2)}) async-start(), calls=%async_computation.4 | async-start | bytes 2621440 | tf_op jit(solution)/shard_map/all_gather | solution.py:74
  100.0 174.8 %reduce-scatter.2.cloned.1.call-start = ((), (), s32[]{:S(2)}) async-start(), calls=%async_computation.2 | async-start | bytes 4718592 | tf_op jit(solution)/shard_map/reduce_scatter | solution.py:126
  176.5 2.2 copy-start.1
  182.4 2.2 copy-start.1
  188.4 2.2 copy-start.1
  194.3 2.2 copy-start.1
  225.8 49.0 %copy-start = (bf16[64,4096]{1,0:T(8,128)(2,1)S(1)}, bf16[64,4096]{1,0:T(8,128)(2,1)}, u32[]{:S(2)}) copy-start(bf16[64,4096]{1,0:T(8,128)(2,1)} %param.14) | copy-start | bytes 1572868
Sparse Core Ops, SparseCore 0:
  12.1 47.1 all-gather.5
  99.4 34.5 all-gather.7
  135.8 35.0 all-gather.9
  226.0 48.8 reduce-scatter.1
where the time goes:
time: 287 us; the launch traced here: 283 us
  waiting for transfers between devices  164 us (57%)
  matrix products  51.3 us (18%)
  local copies, waits for them, and re-layouts  18.7 us (7%)
  loops' own time  18.6 us (6%)
  other arithmetic  17.4 us (6%)
  between operations  13.3 us (5%)
    reduce_scatter x1, waiting for transfers between devices, body(): lax.psum_scatter(partial_value.reshape(group_rows, partial_value.shape[2]...  49 us
    all_gather x1, waiting for transfers between devices, body(): gathered = lax.all_gather(normed, 'seq', axis=0, tiled=True)  47.1 us
    all_gather x1, waiting for transfers between devices, body(): piece_values = lax.all_gather(values_here, 'mod', axis=0, tiled=True)  33.9 us
    all_gather x1, waiting for transfers between devices, body(): piece_keys = lax.all_gather(keys_here, 'mod', axis=0, tiled=True)  33.1 us
    dot_general x4, matrix products, project(): jnp.dot(row_block, weight, preferred_element_type=jnp.float32)  26.9 us
    dot_general x4, matrix products, output(): return jnp.dot(row_block, weight, preferred_element_type=jnp.float32)  15.8 us
    another operation x1, loops' own time, body(): lax.map(project, (gathered.reshape(block_count, BLOCK, gathered.shape[1])...  7.85 us
    another operation x1, loops' own time, body(): lax.map(output, (attended.reshape(block_count, BLOCK, attended.shape[1]),...  7.79 us
  transfers between devices with their start and end apart: 4, of which 4 were waited for; matrix products, arithmetic and copies ran while one was open for 1% of the time, Pallas kernels for 0%

commit v1 on v0

v1 whole, which is shorter than its diff:
```python
import functools
import math

import jax
import jax.numpy as jnp
from jax import lax
from jax.experimental import pallas as pl
from jax.experimental.pallas import tpu as pltpu
from jax.sharding import PartitionSpec as P

HDIM = 128
MESH = pl.DeviceIdType.MESH
F32 = jnp.float32
BF16 = jnp.bfloat16


def mul(x, k):
    return pl.multiple_of(x, k)


def remote(src, dst, send, recv, dev):
    return pltpu.make_async_remote_copy(
        src_ref=src, dst_ref=dst, send_sem=send, recv_sem=recv,
        device_id=dev, device_id_type=MESH,
    )


def greet(devs):
    barrier = pltpu.get_barrier_semaphore()
    for dev in devs:
        pl.semaphore_signal(barrier, inc=1, device_id=dev, device_id_type=MESH)
    pl.semaphore_wait(barrier, len(devs))


def gather_project(
    n, modality, tokens, gain, w_hbm, q_out, kv_out, wv, xg, stage,
    w_sem, rs, rr, ls, lr, ps, pr, a_s, a_r, b_s, b_r,
):
    m = lax.axis_index("mod")
    s = lax.axis_index("seq")
    chip, core = s // 2, s % 2
    rows, width = tokens.shape
    pair = 2 * rows
    group = n * pair
    half = n // 2
    feats = q_out.shape[1]
    heads = feats // HDIM
    mods = w_hbm.shape[0]
    right = (m, ((chip + 1) % n) * 2 + core)
    left = (m, ((chip + n - 1) % n) * 2 + core)
    partner = (m, chip * 2 + (1 - core))

    w_copies = [pltpu.make_async_copy(w_hbm.at[k], wv.at[k], w_sem.at[k]) for k in range(mods)]
    for c in w_copies:
        c.start()

    def block_rows(offset):
        return mul(((chip + offset + n) % n) * pair, pair)

    def at(offset, which, first=0, count=rows):
        return xg.at[pl.ds(mul(block_rows(offset) + which * rows + first, count), count), :]

    values = tokens[...].astype(F32)
    inv = lax.rsqrt(jnp.mean(values * values, axis=1, keepdims=True) + 1e-05)
    row_gain = gain[pl.ds(modality[m * n + chip], 1), :]
    xg[pl.ds(mul(block_rows(0) + core * rows, rows), rows), :] = (values * inv * row_gain).astype(BF16)

    @pl.when(m < 2)
    def _():
        kv_out[pl.ds(0, group), :] = jnp.zeros((group, 2 * feats), BF16)

    @pl.when(m < 1)
    def _():
        kv_out[pl.ds(group, group), :] = jnp.zeros((group, 2 * feats), BF16)

    others = [((m + d) % 4, s) for d in range(1, 4)]
    greet([right, left, partner] + others)

    def going(k, part, to, ssem, rsem, sign):
        off = -sign * (k - 1)
        if part is None:
            ref = at(off, core)
        else:
            ref = at(off, core, part * (rows // 2), rows // 2)
        return remote(ref, ref, ssem.at[k - 1], rsem.at[k - 1], to)

    def right_copy(k):
        return going(k, 0 if k == half else None, right, rs, rr, 1)

    def left_copy(k):
        return going(k, 1 if k == half else None, left, ls, lr, -1)

    def landed(k, sign, rsem, ssem):
        off = -sign * k
        if k == half:
            ref = at(off, core, (0 if sign > 0 else rows // 2), rows // 2)
        else:
            ref = at(off, core)
        return remote(ref, ref, ssem.at[k - 1], rsem.at[k - 1], right)

    def partner_copy(off, which):
        ref = at(off, core)
        return remote(ref, ref, ps.at[which], pr.at[which], partner)

    def partner_landed(off, which):
        ref = at(off, 1 - core)
        return remote(ref, ref, ps.at[which], pr.at[which], partner)

    sent = []

    def go(copy):
        copy.start()
        sent.append(copy)

    go(right_copy(1))
    go(left_copy(1))
    go(partner_copy(0, 0))

    tile = 256 if (3 * feats) % 256 == 0 else 128

    def own_copies(t, r):
        src = kv_out.at[pl.ds(mul(2 * group + r, pair), pair), :]
        near = kv_out.at[pl.ds(mul(group + r, pair), pair), :]
        far = kv_out.at[pl.ds(r, pair), :]
        return {
            0: [remote(src, near, a_s.at[t], a_r.at[t], (1, s)), remote(src, far, b_s.at[t], b_r.at[t], (2, s))],
            1: [remote(src, far, b_s.at[t], b_r.at[t], (3, s))],
            2: [remote(src, near, a_s.at[t], a_r.at[t], (3, s))],
            3: [remote(far, near, a_s.at[t], a_r.at[t], (2, s))],
        }

    plan = []

    def project(off):
        t = len(plan)
        r = block_rows(off)
        mode = modality[m * n + (chip + off + n) % n]

        def one_tile(j, carry):
            cols = pl.ds(mul(j * tile, tile), tile)
            stage[:, cols] = jnp.dot(
                xg[pl.ds(r, pair), :], wv[mode, :, cols], preferred_element_type=F32
            ).astype(BF16)
            return carry

        lax.fori_loop(0, 3 * feats // tile, one_tile, 0)
        for h in range(heads):
            q_out[pl.ds(r, pair), pl.ds(h * HDIM, HDIM)] = stage[:, pl.ds(3 * h * HDIM, HDIM)]
            kv_out[pl.ds(mul(2 * group + r, pair), pair), pl.ds(2 * h * HDIM, 2 * HDIM)] = stage[
                :, pl.ds((3 * h + 1) * HDIM, 2 * HDIM)
            ]
        copies = own_copies(t, r)
        plan.append(copies)
        for who in range(3):
            @pl.when(m == who)
            def _(who=who):
                for c in copies[who]:
                    c.start()
        forward_to(t)

    forwarded = []

    def forward_to(count):
        for t in range(len(forwarded), count):
            forwarded.append(t)

            @pl.when(m == 3)
            def _(t=t):
                plan[t][1][0].wait_recv()
                plan[t][3][0].start()

    for c in w_copies:
        c.wait()
    next_pair = 1
    for k in range(1, half):
        landed(k, 1, rr, rs).wait_recv()
        go(right_copy(k + 1))
        landed(k, -1, lr, ls).wait_recv()
        go(left_copy(k + 1))
        go(partner_copy(-k, next_pair))
        go(partner_copy(k, next_pair + 1))
        if k == 1:
            partner_landed(0, 0).wait_recv()
            project(0)
        partner_landed(-k, next_pair).wait_recv()
        project(-k)
        if k == half - 1:
            landed(half, 1, rr, rs).wait_recv()
            landed(half, -1, lr, ls).wait_recv()
            go(partner_copy(half, next_pair + 2))
        partner_landed(k, next_pair + 1).wait_recv()
        project(k)
        next_pair += 2
    partner_landed(half, next_pair).wait_recv()
    project(half)
    forward_to(n)
    for copy in sent:
        copy.wait_send()
    for who in range(4):
        @pl.when(m == who)
        def _(who=who):
            for copies in plan:
                for c in copies[who]:
                    c.wait_send()
                if who in (1, 3):
                    copies[0 if who == 1 else 2][0].wait_recv()
                if who == 2:
                    copies[3][0].wait_recv()
                    copies[0][1].wait_recv()


def attend_reduce(
    n, modality, doc_lengths, tokens, q, kv, w_hbm, out, wv, att, part, pairbuf, bias, right_in, left_in,
    w_sem, ps, pr, rs, rr, ls, lr,
):
    m = lax.axis_index("mod")
    s = lax.axis_index("seq")
    chip, core = s // 2, s % 2
    rows, width = tokens.shape
    pair = 2 * rows
    group = n * pair
    half = n // 2
    feats = q.shape[1]
    heads = feats // HDIM
    mods = w_hbm.shape[0]
    right = (m, ((chip + 1) % n) * 2 + core)
    left = (m, ((chip + n - 1) % n) * 2 + core)
    partner = (m, chip * 2 + (1 - core))
    w_copies = [pltpu.make_async_copy(w_hbm.at[k], wv.at[k], w_sem.at[k]) for k in range(mods)]
    for c in w_copies:
        c.start()
    greet([right, left, partner])

    keys = 3 * group
    chunk = keys
    while chunk > 1536:
        chunk //= 2
    scale = math.log2(math.e) / math.sqrt(HDIM)
    first_key = (m - 2) * group
    mine = pl.ds(mul(core * rows, rows), rows)
    theirs = pl.ds(mul((1 - core) * rows, rows), rows)
    waited = []

    def compute(t, off):
        r = mul(((chip + off + n) % n) * pair, pair)
        pos = m * group + r + lax.broadcasted_iota(jnp.int32, (pair, 1), 0)
        end = jnp.int32(0)
        start = jnp.zeros((pair, 1), jnp.int32)
        for d in range(doc_lengths.shape[0]):
            end = end + doc_lengths[d]
            start = jnp.where(pos >= end, end, start)
        for c0 in range(0, keys, chunk):
            key = first_key + c0 + lax.broadcasted_iota(jnp.int32, (pair, chunk), 1)
            bias[:, pl.ds(c0, chunk)] = jnp.where((key <= pos) & (key >= start), 0.0, -1e30)
        for h in range(heads):
            query = q[pl.ds(r, pair), pl.ds(h * HDIM, HDIM)]
            top = total = acc = None
            for c0 in reversed(range(0, keys, chunk)):
                k_part = kv[pl.ds(c0, chunk), pl.ds(2 * h * HDIM, HDIM)]
                v_part = kv[pl.ds(c0, chunk), pl.ds((2 * h + 1) * HDIM, HDIM)]
                scores = lax.dot_general(
                    query, k_part, (((1,), (1,)), ((), ())), preferred_element_type=F32
                ) * scale + bias[:, pl.ds(c0, chunk)]
                peak = jnp.max(scores, axis=1, keepdims=True)
                new_top = peak if top is None else jnp.maximum(top, peak)
                weights = jnp.exp2(scores - new_top)
                if chunk != keys:
                    weights = jnp.where(bias[:, pl.ds(c0, chunk)] < 0.0, 0.0, weights)
                row_sum = jnp.sum(weights, axis=1, keepdims=True)
                added = jnp.dot(weights.astype(BF16), v_part, preferred_element_type=F32)
                if top is None:
                    total, acc = row_sum, added
                else:
                    fix = jnp.exp2(top - new_top)
                    total, acc = total * fix + row_sum, acc * fix + added
                top = new_top
            att[:, pl.ds(h * HDIM, HDIM)] = (acc / total).astype(BF16)
        if not waited:
            for c in w_copies:
                c.wait()
            waited.append(True)
        mode = modality[m * n + (chip + off + n) % n]
        tile = 512

        def one_tile(j, carry):
            cols = pl.ds(mul(j * tile, tile), tile)
            part[t, :, cols] = jnp.dot(
                att[...], wv[mode, :, cols], preferred_element_type=F32
            ).astype(BF16)
            return carry

        lax.fori_loop(0, width // tile, one_tile, 0)
        copy = remote(part.at[t, theirs, :], pairbuf.at[t], ps.at[t], pr.at[t], partner)
        copy.start()
        return copy

    lo, hi = pl.ds(0, width // 2), pl.ds(width // 2, width // 2)
    sent = []

    def pair_sum(t, copy):
        copy.wait_recv()
        sent.append(copy)
        return part[t, mine, :].astype(F32) + pairbuf[t].astype(F32)

    def send(src, dst, ss, rsm, dev):
        copy = remote(src, dst, ss, rsm, dev)
        copy.start()
        sent.append(copy)
        return copy

    copy = compute(0, half)
    part[0, mine, :] = pair_sum(0, copy).astype(BF16)
    r_prev = send(part.at[0, mine, lo], right_in.at[half - 1, :, lo], rs.at[half - 1], rr.at[half - 1], right)
    l_prev = send(part.at[0, mine, hi], left_in.at[half - 1, :, hi], ls.at[half - 1], lr.at[half - 1], left)
    t = 1
    for k in range(half - 1, 0, -1):
        c_right = compute(t, k)
        c_left = compute(t + 1, -k)
        for which, (tt, c, prev, inbox, ss, rsm, dev, cols) in enumerate((
            (t, c_right, r_prev, right_in, rs, rr, right, lo),
            (t + 1, c_left, l_prev, left_in, ls, lr, left, hi),
        )):
            total = pair_sum(tt, c)
            prev.wait_recv()
            if k == half - 1:
                a, b = total[:, : width // 2], total[:, width // 2:]
                if which == 0:
                    a = a + inbox[k, :, lo].astype(F32)
                else:
                    b = b + inbox[k, :, hi].astype(F32)
                part[tt, mine, lo] = a.astype(BF16)
                part[tt, mine, hi] = b.astype(BF16)
            else:
                part[tt, mine, :] = (total + inbox[k].astype(F32)).astype(BF16)
            new = send(part.at[tt, mine, :], inbox.at[k - 1], ss.at[k - 1], rsm.at[k - 1], dev)
            if which == 0:
                r_prev = new
            else:
                l_prev = new
        t += 2
    c = compute(t, 0)
    total = pair_sum(t, c) + tokens[...].astype(F32)
    r_prev.wait_recv()
    total = total + right_in[0].astype(F32)
    l_prev.wait_recv()
    out[...] = (total + left_in[0].astype(F32)).astype(BF16)
    for copy in sent:
        copy.wait_send()


def body(n, tokens, norm_gain, qkv_weight, out_weight, modality, doc_lengths):
    rows, width = tokens.shape
    feats = out_weight.shape[1]
    mods = out_weight.shape[0]
    pair = 2 * rows
    group = n * pair
    half = n // 2
    vmem = pl.BlockSpec(memory_space=pltpu.VMEM)
    smem = pl.BlockSpec(memory_space=pltpu.SMEM)
    hbm = pl.BlockSpec(memory_space=pl.ANY)
    dma = pltpu.SemaphoreType.DMA
    limit = 62 * 1024 * 1024
    q, kv = pl.pallas_call(
        functools.partial(gather_project, n),
        out_shape=(
            jax.ShapeDtypeStruct((group, feats), BF16),
            jax.ShapeDtypeStruct((3 * group, 2 * feats), BF16),
        ),
        in_specs=[smem, vmem, vmem, hbm],
        out_specs=(vmem, vmem),
        scratch_shapes=[
            pltpu.VMEM((mods, width, 3 * feats), BF16),
            pltpu.VMEM((group, width), BF16),
            pltpu.VMEM((pair, 3 * feats), BF16),
            dma((mods,)),
            dma((half,)), dma((half,)), dma((half,)), dma((half,)),
            dma((n,)), dma((n,)),
            dma((n,)), dma((n,)), dma((n,)), dma((n,)),
        ],
        compiler_params=pltpu.CompilerParams(
            collective_id=0, has_side_effects=True, vmem_limit_bytes=limit
        ),
    )(modality, tokens, norm_gain, qkv_weight)
    return pl.pallas_call(
        functools.partial(attend_reduce, n),
        out_shape=jax.ShapeDtypeStruct((rows, width), BF16),
        in_specs=[smem, smem, vmem, vmem, vmem, hbm],
        out_specs=vmem,
        scratch_shapes=[
            pltpu.VMEM((mods, feats, width), BF16),
            pltpu.VMEM((pair, feats), BF16),
            pltpu.VMEM((n, pair, width), BF16),
            pltpu.VMEM((n, rows, width), BF16),
            pltpu.VMEM((pair, 3 * group), F32),
            pltpu.VMEM((half, rows, width), BF16),
            pltpu.VMEM((half, rows, width), BF16),
            dma((mods,)),
            dma((n,)), dma((n,)),
            dma((half,)), dma((half,)), dma((half,)), dma((half,)),
        ],
        compiler_params=pltpu.CompilerParams(
            collective_id=1, has_side_effects=True, vmem_limit_bytes=limit
        ),
    )(modality, doc_lengths, tokens, q, kv, out_weight)


def solution(mesh):
    return jax.shard_map(
        functools.partial(body, mesh.shape["seq"] // 2),
        mesh=mesh,
        in_specs=(
            P(("mod", "seq"), None),
            P(),
            P(None, None, "seq"),
            P(None, "seq", None),
            P(),
            P(),
        ),
        out_specs=P(("mod", "seq"), None),
        check_vma=False,
    )
```

time: 287 us -> 115 us (0.40)
  waiting for transfers between devices: 164 us -> 0 us
  Pallas kernels: 0 us -> 112 us
  matrix products: 51.3 us -> 0 us
  loops' own time: 18.6 us -> 0 us
  other arithmetic: 17.4 us -> 0 us
  local copies, waits for them, and re-layouts: 18.7 us -> 1.87 us
  between operations: 13.3 us -> 0.02 us
    all_gather x3 -> x0, waiting for transfers between devices: 114 us -> none  [the longest x1 47.1 us: body(): gathered = lax.all_gather(normed, 'seq', axis=0, tiled=True)]
    pallas_call x0 -> x2, Pallas kernels: none -> 112 us  [the longest x1 62.4 us: body(): pl.pallas_call(functools.partial(gather_project, n), out_shape=(jax.Shape...]
    dot_general x16 -> x0, matrix products: 51.3 us -> none  [the longest x4 26.9 us: project(): jnp.dot(row_block, weight, preferred_element_type=jnp.float32)]
    reduce_scatter x1 -> x0, waiting for transfers between devices: 49 us -> none  [body(): lax.psum_scatter(partial_value.reshape(group_rows, partial_value.shape[2]...]
    another operation x7 -> x0, loops' own time: 18.6 us -> none  [the longest x1 7.85 us: body(): lax.map(project, (gathered.reshape(block_count, BLOCK, gathered.shape[1])...]
    reduce_sum x9 -> x0, other arithmetic: 8.16 us -> none  [the longest x4 4.63 us: attend(): new_totals = totals * rescale + jnp.sum(weights, axis=2)]
    convert_element_type x3 -> x0, other arithmetic: 5.33 us -> none  [the longest x1 2.03 us: body(): (values * lax.rsqrt(mean_square + 1e-05) * gain_rows).astype(jnp.bfloat16)]
    unnamed x9 -> x1, local copies, waits for them, and re-layouts: 7.05 us -> 1.87 us
  transfers between devices with their start and end apart: 4 -> 0, of which waited for: 4 -> 0; matrix products, arithmetic and copies ran while one was open for 1% -> 0% of each run, Pallas kernels for 0% -> 0%
where the time goes in v1:
time: 115 us; the launch traced here: 114 us
  Pallas kernels  112 us (97%)
  local copies, waits for them, and re-layouts  1.87 us (2%)
    pallas_call x1, Pallas kernels, body(): pl.pallas_call(functools.partial(gather_project, n), out_shape=(jax.Shape...  62.4 us
    pallas_call x1, Pallas kernels, body(): pl.pallas_call(functools.partial(attend_reduce, n), out_shape=jax.ShapeDt...  49.8 us

profile of v1, /device:TPU:13, one launch (start us, length us, event | category | flops | bytes accessed | tf_op | source)
XLA Modules:
  0.0 114.1 jit_solution(11207395065083084446)
XLA Ops:
  0.0 62.4 %shard_map.64 = (bf16[512,512]{1,0:T(8,128)(2,1)}, bf16[1536,1024]{1,0:T(8,128)(2,1)}) custom-call(s32[16]{0:T(128)} %modality.3, bf16[64,4096]{1,0:T(8,128)(2,1)} %tokens.3, f32[3,4096]{1,0:T(4,128)} %gain.1, bf16[3,4096,1536]{2,1,0:T(8,128)(2,1)} %w_hbm.2), custom_call_target="tpu_custom_call" | custom-call | tf_op jit(solution)/shard_map/pallas_call | solution.py:363
  62.4 49.8 %shard_map.65 = bf16[64,4096]{1,0:T(8,128)(2,1)} custom-call(s32[16]{0:T(128)} %modality.3, s32[4]{0:T(128)} %doc_lengths.1, bf16[64,4096]{1,0:T(8,128)(2,1)} %tokens.3, bf16[512,512]{1,0:T(8,128)(2,1)} %get-tuple-element.7.q, bf16[1536,1024]{1,0:T(8,128)(2,1)} %get-tuple-element.8.kv, bf16[3,512,4096]{2,1,0:T(8,128)(2,1)} %w_hbm.3), custom_call_target="tpu_custom_call" | custom-call | tf_op jit(solution)/shard_map/pallas_call | solution.py:384
  112.2 1.9 %copy.8 = bf16[64,4096]{1,0:T(8,128)(2,1)} copy(bf16[64,4096]{1,0:T(8,128)(2,1)} %shard_map.65) | data formatting | bytes 1048576

commit v2 on v1

v2 whole, which is shorter than its diff:
```python
import functools
import math

import jax
import jax.numpy as jnp
from jax import lax
from jax.experimental import pallas as pl
from jax.experimental.pallas import tpu as pltpu
from jax.sharding import PartitionSpec as P

HDIM = 128
MESH = pl.DeviceIdType.MESH
F32 = jnp.float32
BF16 = jnp.bfloat16


def mul(x, k):
    return pl.multiple_of(x, k)


def remote(src, dst, send, recv, dev):
    return pltpu.make_async_remote_copy(
        src_ref=src, dst_ref=dst, send_sem=send, recv_sem=recv,
        device_id=dev, device_id_type=MESH,
    )


def greet(devs):
    barrier = pltpu.get_barrier_semaphore()
    for dev in devs:
        pl.semaphore_signal(barrier, inc=1, device_id=dev, device_id_type=MESH)
    pl.semaphore_wait(barrier, len(devs))


def sublayer(
    n, modality, doc_lengths, tokens, gain, w_hbm, o_hbm, out,
    wv, xg, stage, q_out, kv_out, att, pairbuf, bias, right_in, left_in,
    w_sem, o_sem, own_s, fs, fr, ps, pr, a_s, a_r, b_s, b_r, ps2, pr2, rs, rr, ls, lr,
):
    m = lax.axis_index("mod")
    s = lax.axis_index("seq")
    chip, core = s // 2, s % 2
    rows, width = tokens.shape
    pair = 2 * rows
    group = n * pair
    half = n // 2
    feats = q_out.shape[1]
    heads = feats // HDIM
    mods = w_hbm.shape[0]
    right = (m, ((chip + 1) % n) * 2 + core)
    left = (m, ((chip + n - 1) % n) * 2 + core)
    partner = (m, chip * 2 + (1 - core))
    chunks = 2
    piece = rows // chunks

    w_copies = [pltpu.make_async_copy(w_hbm.at[k], wv.at[k], w_sem.at[k]) for k in range(mods)]
    for c in w_copies:
        c.start()

    values = tokens[...].astype(F32)
    inv = lax.rsqrt(jnp.mean(values * values, axis=1, keepdims=True) + 1e-05)
    row_gain = gain[pl.ds(modality[m * n + chip], 1), :]
    xg[pl.ds(mul(chip * pair + core * rows, rows), rows), :] = (values * inv * row_gain).astype(BF16)

    @pl.when(m < 2)
    def _():
        kv_out[pl.ds(0, group), :] = jnp.zeros((group, 2 * feats), BF16)

    @pl.when(m < 1)
    def _():
        kv_out[pl.ds(group, group), :] = jnp.zeros((group, 2 * feats), BF16)

    others = [((m + d) % 4, s) for d in range(1, 4)]
    greet([right, left, partner] + others)

    def ref(block, which, c):
        return xg.at[pl.ds(mul(block * pair + which * rows + c * piece, piece), piece), :]

    def to_partner(block, c):
        r = ref(block, core, c)
        return remote(r, r, ps.at[block, c], pr.at[block, c], partner)

    def from_partner(block, c):
        r = ref(block, 1 - core, c)
        return remote(r, r, ps.at[block, c], pr.at[block, c], partner)

    def onward(block, c, dev, sem):
        r = ref(block, core, c)
        return remote(r, r, sem, fr.at[block, c], dev)

    for c in range(chunks):
        @pl.when(chip < n - 1)
        def _(c=c):
            onward(chip, c, right, own_s.at[0, c]).start()

        @pl.when(chip > 0)
        def _(c=c):
            onward(chip, c, left, own_s.at[1, c]).start()
    for c in range(chunks):
        to_partner(chip, c).start()

    def handle(k, c):
        for sign, dev in ((-1, right), (1, left)):
            block = chip + sign * k
            following = chip - sign

            @pl.when((block >= 0) & (block < n))
            def _(block=block, following=following, dev=dev):
                onward(block, c, dev, fs.at[block, c]).wait_recv()

                @pl.when((following >= 0) & (following < n))
                def _():
                    onward(block, c, dev, fs.at[block, c]).start()

                to_partner(block, c).start()

    def settle():
        for c in range(chunks):
            @pl.when(chip < n - 1)
            def _(c=c):
                onward(chip, c, right, own_s.at[0, c]).wait_send()

            @pl.when(chip > 0)
            def _(c=c):
                onward(chip, c, left, own_s.at[1, c]).wait_send()

            for d in range(n):
                to_partner((chip + d) % n, c).wait_send()
            for k in range(1, n):
                for sign, dev in ((-1, right), (1, left)):
                    block = chip + sign * k
                    following = chip - sign

                    @pl.when((block >= 0) & (block < n) & (following >= 0) & (following < n))
                    def _(block=block, dev=dev, c=c):
                        onward(block, c, dev, fs.at[block, c]).wait_send()

    tile = 256 if (3 * feats) % 256 == 0 else 128
    upper = chip // half
    near_side = chip * (1 - upper) + (n - 1 - chip) * upper
    far_sign = 1 - 2 * upper

    def block_at(t):
        if t == 0:
            return chip
        step = (t + 1) // 2
        two = step if t % 2 == 0 else -step
        past = (t - 1 - 2 * near_side + 2 * n) // (2 * n)
        return chip + two * (1 - past) + far_sign * (t - near_side) * past

    def own_copies(t, r):
        src = kv_out.at[pl.ds(mul(2 * group + r, pair), pair), :]
        near = kv_out.at[pl.ds(mul(group + r, pair), pair), :]
        far = kv_out.at[pl.ds(r, pair), :]
        return {
            0: [remote(src, near, a_s.at[t], a_r.at[t], (1, s)), remote(src, far, b_s.at[t], b_r.at[t], (2, s))],
            1: [remote(src, far, b_s.at[t], b_r.at[t], (3, s))],
            2: [remote(src, near, a_s.at[t], a_r.at[t], (3, s))],
            3: [remote(far, near, a_s.at[t], a_r.at[t], (2, s))],
        }

    plan = []
    forwarded = []

    def forward_to(count):
        for t in range(len(forwarded), count):
            forwarded.append(t)

            @pl.when(m == 3)
            def _(t=t):
                plan[t][1][0].wait_recv()
                plan[t][3][0].start()

    def project():
        t = len(plan)
        block = block_at(t)
        r = mul(block * pair, pair)
        mode = modality[m * n + block]
        for c in range(chunks):
            from_partner(block, c).wait_recv()

        def one_tile(j, carry):
            cols = pl.ds(mul(j * tile, tile), tile)
            stage[:, cols] = jnp.dot(
                xg[pl.ds(r, pair), :], wv[mode, :, cols], preferred_element_type=F32
            ).astype(BF16)
            return carry

        lax.fori_loop(0, 3 * feats // tile, one_tile, 0)
        for h in range(heads):
            q_out[pl.ds(r, pair), pl.ds(h * HDIM, HDIM)] = stage[:, pl.ds(3 * h * HDIM, HDIM)]
            kv_out[pl.ds(mul(2 * group + r, pair), pair), pl.ds(2 * h * HDIM, 2 * HDIM)] = stage[
                :, pl.ds((3 * h + 1) * HDIM, 2 * HDIM)
            ]
        copies = own_copies(t, r)
        plan.append(copies)
        for who in range(3):
            @pl.when(m == who)
            def _(who=who):
                for c in copies[who]:
                    c.start()
        forward_to(t)

    for c in range(chunks - 1):
        handle(1, c)
    for c in w_copies:
        c.wait()
    project()
    handle(1, chunks - 1)
    project()
    for k in range(2, n):
        for c in range(chunks):
            handle(k, c)
        project()
    squares = width // feats
    o_copies = [
        pltpu.make_async_copy(
            o_hbm.at[k, :, pl.ds(c * feats, feats)],
            wv.at[k, pl.ds(c * feats, feats), pl.ds(0, feats)],
            o_sem.at[k * squares + c],
        )
        for c in range(squares) for k in range(mods)
    ]
    for c in o_copies:
        c.start()
    forward_to(n)
    settle()
    for who in range(4):
        @pl.when(m == who)
        def _(who=who):
            for copies in plan:
                if who in (1, 3):
                    copies[0 if who == 1 else 2][0].wait_recv()
                if who == 2:
                    copies[3][0].wait_recv()
                    copies[0][1].wait_recv()

    q, kv = q_out, kv_out
    keys = 3 * group
    chunk = keys
    while chunk > 1536:
        chunk //= 2
    scale = math.log2(math.e) / math.sqrt(HDIM)
    first_key = (m - 2) * group
    def mine(t):
        return pl.ds(mul(t * pair + core * rows, rows), rows)

    def theirs(t):
        return pl.ds(mul(t * pair + (1 - core) * rows, rows), rows)

    waited = []

    def compute(t, off):
        r = mul(((chip + off + n) % n) * pair, pair)
        pos = m * group + r + lax.broadcasted_iota(jnp.int32, (pair, 1), 0)
        end = jnp.int32(0)
        start = jnp.zeros((pair, 1), jnp.int32)
        for d in range(doc_lengths.shape[0]):
            end = end + doc_lengths[d]
            start = jnp.where(pos >= end, end, start)
        for c0 in range(0, keys, chunk):
            key = first_key + c0 + lax.broadcasted_iota(jnp.int32, (pair, chunk), 1)
            bias[:, pl.ds(c0, chunk)] = jnp.where((key <= pos) & (key >= start), 0.0, -1e30)
        for h in range(heads):
            query = q[pl.ds(r, pair), pl.ds(h * HDIM, HDIM)]
            top = total = acc = None
            for c0 in reversed(range(0, keys, chunk)):
                k_part = kv[pl.ds(c0, chunk), pl.ds(2 * h * HDIM, HDIM)]
                v_part = kv[pl.ds(c0, chunk), pl.ds((2 * h + 1) * HDIM, HDIM)]
                scores = lax.dot_general(
                    query, k_part, (((1,), (1,)), ((), ())), preferred_element_type=F32
                ) * scale + bias[:, pl.ds(c0, chunk)]
                peak = jnp.max(scores, axis=1, keepdims=True)
                new_top = peak if top is None else jnp.maximum(top, peak)
                weights = jnp.exp2(scores - new_top)
                if chunk != keys:
                    weights = jnp.where(bias[:, pl.ds(c0, chunk)] < 0.0, 0.0, weights)
                row_sum = jnp.sum(weights, axis=1, keepdims=True)
                added = jnp.dot(weights.astype(BF16), v_part, preferred_element_type=F32)
                if top is None:
                    total, acc = row_sum, added
                else:
                    fix = jnp.exp2(top - new_top)
                    total, acc = total * fix + row_sum, acc * fix + added
                top = new_top
            att[:, pl.ds(h * HDIM, HDIM)] = (acc / total).astype(BF16)
        if not waited:
            for c in o_copies:
                c.wait()
            waited.append(True)
        mode = modality[m * n + (chip + off + n) % n]

        def one_tile(j, carry):
            cols = pl.ds(mul(j * feats, feats), feats)
            square = wv[mode, cols, pl.ds(0, feats)]
            xg[pl.ds(t * pair, pair), cols] = jnp.dot(
                att[...], square, preferred_element_type=F32
            ).astype(BF16)
            return carry

        lax.fori_loop(0, squares, one_tile, 0)
        copy = remote(xg.at[theirs(t), :], pairbuf.at[t], ps2.at[t], pr2.at[t], partner)
        copy.start()
        return copy

    lo, hi = pl.ds(0, width // 2), pl.ds(width // 2, width // 2)
    sent = []

    def pair_sum(t, copy):
        copy.wait_recv()
        sent.append(copy)
        return xg[mine(t), :].astype(F32) + pairbuf[t].astype(F32)

    def send(src, dst, ss, rsm, dev):
        copy = remote(src, dst, ss, rsm, dev)
        copy.start()
        sent.append(copy)
        return copy

    copy = compute(0, half)
    xg[mine(0), :] = pair_sum(0, copy).astype(BF16)
    r_prev = send(xg.at[mine(0), lo], right_in.at[half - 1, :, lo], rs.at[half - 1], rr.at[half - 1], right)
    l_prev = send(xg.at[mine(0), hi], left_in.at[half - 1, :, hi], ls.at[half - 1], lr.at[half - 1], left)
    t = 1
    for k in range(half - 1, 0, -1):
        c_right = compute(t, k)
        c_left = compute(t + 1, -k)
        for which, (tt, c, prev, inbox, ss, rsm, dev, cols) in enumerate((
            (t, c_right, r_prev, right_in, rs, rr, right, lo),
            (t + 1, c_left, l_prev, left_in, ls, lr, left, hi),
        )):
            total = pair_sum(tt, c)
            prev.wait_recv()
            if k == half - 1:
                a, b = total[:, : width // 2], total[:, width // 2:]
                if which == 0:
                    a = a + inbox[k, :, lo].astype(F32)
                else:
                    b = b + inbox[k, :, hi].astype(F32)
                xg[mine(tt), lo] = a.astype(BF16)
                xg[mine(tt), hi] = b.astype(BF16)
            else:
                xg[mine(tt), :] = (total + inbox[k].astype(F32)).astype(BF16)
            new = send(xg.at[mine(tt), :], inbox.at[k - 1], ss.at[k - 1], rsm.at[k - 1], dev)
            if which == 0:
                r_prev = new
            else:
                l_prev = new
        t += 2
    c = compute(t, 0)
    total = pair_sum(t, c) + tokens[...].astype(F32)
    r_prev.wait_recv()
    total = total + right_in[0].astype(F32)
    l_prev.wait_recv()
    out[...] = (total + left_in[0].astype(F32)).astype(BF16)
    for copy in sent:
        copy.wait_send()


    for who in range(4):
        @pl.when(m == who)
        def _(who=who):
            for copies in plan:
                for c in copies[who]:
                    c.wait_send()


def body(n, tokens, norm_gain, qkv_weight, out_weight, modality, doc_lengths):
    rows, width = tokens.shape
    feats = out_weight.shape[1]
    mods = out_weight.shape[0]
    pair = 2 * rows
    group = n * pair
    half = n // 2
    vmem = pl.BlockSpec(memory_space=pltpu.VMEM)
    smem = pl.BlockSpec(memory_space=pltpu.SMEM)
    hbm = pl.BlockSpec(memory_space=pl.ANY)
    dma = pltpu.SemaphoreType.DMA
    limit = 62 * 1024 * 1024
    return pl.pallas_call(
        functools.partial(sublayer, n),
        out_shape=jax.ShapeDtypeStruct((rows, width), BF16),
        in_specs=[smem, smem, vmem, vmem, hbm, hbm],
        out_specs=vmem,
        scratch_shapes=[
            pltpu.VMEM((mods, width, 3 * feats), BF16),
            pltpu.VMEM((group, width), BF16),
            pltpu.VMEM((pair, 3 * feats), BF16),
            pltpu.VMEM((group, feats), BF16),
            pltpu.VMEM((3 * group, 2 * feats), BF16),
            pltpu.VMEM((pair, feats), BF16),
            pltpu.VMEM((n, rows, width), BF16),
            pltpu.VMEM((pair, 3 * group), F32),
            pltpu.VMEM((half, rows, width), BF16),
            pltpu.VMEM((half, rows, width), BF16),
            dma((mods,)), dma((mods * (width // feats),)),
            dma((2, 2)), dma((n, 2)), dma((n, 2)), dma((n, 2)), dma((n, 2)),
            dma((n,)), dma((n,)), dma((n,)), dma((n,)),
            dma((n,)), dma((n,)),
            dma((half,)), dma((half,)), dma((half,)), dma((half,)),
        ],
        compiler_params=pltpu.CompilerParams(
            collective_id=0, has_side_effects=True, vmem_limit_bytes=limit
        ),
    )(modality, doc_lengths, tokens, norm_gain, qkv_weight, out_weight)


def solution(mesh):
    return jax.shard_map(
        functools.partial(body, mesh.shape["seq"] // 2),
        mesh=mesh,
        in_specs=(
            P(("mod", "seq"), None),
            P(),
            P(None, None, "seq"),
            P(None, "seq", None),
            P(),
            P(),
        ),
        out_specs=P(("mod", "seq"), None),
        check_vma=False,
    )
```

time: 115 us -> 103 us (0.90)
  Pallas kernels: 112 us -> 101 us
    pallas_call x2 -> x1, Pallas kernels: 112 us -> 101 us  [body(): pl.pallas_call(functools.partial(sublayer, n), out_shape=jax.ShapeDtypeSt...]
where the time goes in v2:
time: 103 us
  Pallas kernels  101 us (98%)
  local copies, waits for them, and re-layouts  1.87 us (2%)
    pallas_call x1, Pallas kernels, body(): pl.pallas_call(functools.partial(sublayer, n), out_shape=jax.ShapeDtypeSt...  101 us

profile of v2, /device:TPU:13, one launch (start us, length us, event | category | flops | bytes accessed | tf_op | source)
XLA Modules:
  0.0 102.9 jit_solution(3577302301188072600)
XLA Ops:
  0.0 101.0 %shard_map.64 = bf16[64,4096]{1,0:T(8,128)(2,1)} custom-call(s32[16]{0:T(128)} %modality.1, s32[4]{0:T(128)} %doc_lengths.1, bf16[64,4096]{1,0:T(8,128)(2,1)} %tokens.1, f32[3,4096]{1,0:T(4,128)} %gain.1, bf16[3,4096,1536]{2,1,0:T(8,128)(2,1)} %w_hbm.1, bf16[3,512,4096]{2,1,0:T(8,128)(2,1)} %o_hbm.1), custom_call_target="tpu_custom_call" | custom-call | tf_op jit(solution)/shard_map/pallas_call | solution.py:380
  101.0 1.9 %copy.8 = bf16[64,4096]{1,0:T(8,128)(2,1)} copy(bf16[64,4096]{1,0:T(8,128)(2,1)} %shard_map.64) | data formatting | bytes 1048576

commit v3 on v2

--- a/solution.py
+++ b/solution.py
@@ -149,15 +149,29 @@
         return chip + two * (1 - past) + far_sign * (t - near_side) * past
 
     def own_copies(t, r):
-        src = kv_out.at[pl.ds(mul(2 * group + r, pair), pair), :]
-        near = kv_out.at[pl.ds(mul(group + r, pair), pair), :]
-        far = kv_out.at[pl.ds(r, pair), :]
+        pieces = 4 if t == n - 1 else 1
+        size = pair // pieces
+
+        def copies(seg_from, seg_to, send, recv, to):
+            return [
+                remote(
+                    kv_out.at[pl.ds(mul(seg_from * group + r + p * size, size), size), :],
+                    kv_out.at[pl.ds(mul(seg_to * group + r + p * size, size), size), :],
+                    send.at[t + p], recv.at[t + p], (to, s),
+                )
+                for p in range(pieces)
+            ]
+
         return {
-            0: [remote(src, near, a_s.at[t], a_r.at[t], (1, s)), remote(src, far, b_s.at[t], b_r.at[t], (2, s))],
-            1: [remote(src, far, b_s.at[t], b_r.at[t], (3, s))],
-            2: [remote(src, near, a_s.at[t], a_r.at[t], (3, s))],
-            3: [remote(far, near, a_s.at[t], a_r.at[t], (2, s))],
+            "near01": copies(2, 1, a_s, a_r, 1),
+            "far02": copies(2, 0, b_s, b_r, 2),
+            "far13": copies(2, 0, b_s, b_r, 3),
+            "near23": copies(2, 1, a_s, a_r, 3),
+            "near32": copies(0, 1, a_s, a_r, 2),
         }
+
+    own_sends = (("near01", "far02"), ("far13",), ("near23",), ("near32",))
+    arrivals = ((), ("near01",), ("near32", "far02"), ("near23",))
 
     plan = []
     forwarded = []
@@ -168,8 +182,9 @@
 
             @pl.when(m == 3)
             def _(t=t):
-                plan[t][1][0].wait_recv()
-                plan[t][3][0].start()
+                for came, goes in zip(plan[t]["far13"], plan[t]["near32"]):
+                    came.wait_recv()
+                    goes.start()
 
     def project():
         t = len(plan)
@@ -197,8 +212,9 @@
         for who in range(3):
             @pl.when(m == who)
             def _(who=who):
-                for c in copies[who]:
-                    c.start()
+                for name in own_sends[who]:
+                    for c in copies[name]:
+                        c.start()
         forward_to(t)
 
     for c in range(chunks - 1):
@@ -229,11 +245,9 @@
         @pl.when(m == who)
         def _(who=who):
             for copies in plan:
-                if who in (1, 3):
-                    copies[0 if who == 1 else 2][0].wait_recv()
-                if who == 2:
-                    copies[3][0].wait_recv()
-                    copies[0][1].wait_recv()
+                for name in arrivals[who]:
+                    for c in copies[name]:
+                        c.wait_recv()
 
     q, kv = q_out, kv_out
     keys = 3 * group
@@ -361,8 +375,9 @@
         @pl.when(m == who)
         def _(who=who):
             for copies in plan:
-                for c in copies[who]:
-                    c.wait_send()
+                for name in own_sends[who]:
+                    for c in copies[name]:
+                        c.wait_send()
 
 
 def body(n, tokens, norm_gain, qkv_weight, out_weight, modality, doc_lengths):
@@ -395,7 +410,7 @@
             pltpu.VMEM((half, rows, width), BF16),
             dma((mods,)), dma((mods * (width // feats),)),
             dma((2, 2)), dma((n, 2)), dma((n, 2)), dma((n, 2)), dma((n, 2)),
-            dma((n,)), dma((n,)), dma((n,)), dma((n,)),
+            dma((n + 3,)), dma((n + 3,)), dma((n + 3,)), dma((n + 3,)),
             dma((n,)), dma((n,)),
             dma((half,)), dma((half,)), dma((half,)), dma((half,)),
         ],

time: 103 us -> 101 us (0.981)
  Pallas kernels: 101 us -> 98.9 us
    pallas_call x1, Pallas kernels: 101 us -> 98.9 us  [body(): pl.pallas_call(functools.partial(sublayer, n), out_shape=jax.ShapeDtypeSt...]
where the time goes in v3:
time: 101 us
  Pallas kernels  98.9 us (98%)
  local copies, waits for them, and re-layouts  1.87 us (2%)
    pallas_call x1, Pallas kernels, body(): pl.pallas_call(functools.partial(sublayer, n), out_shape=jax.ShapeDtypeSt...  98.9 us

profile of v3, /device:TPU:13, one launch (start us, length us, event | category | flops | bytes accessed | tf_op | source)
XLA Modules:
  0.0 100.7 jit_solution(12074562585508852951)
XLA Ops:
  0.0 98.9 %shard_map.64 = bf16[64,4096]{1,0:T(8,128)(2,1)} custom-call(s32[16]{0:T(128)} %modality.1, s32[4]{0:T(128)} %doc_lengths.1, bf16[64,4096]{1,0:T(8,128)(2,1)} %tokens.1, f32[3,4096]{1,0:T(4,128)} %gain.1, bf16[3,4096,1536]{2,1,0:T(8,128)(2,1)} %w_hbm.1, bf16[3,512,4096]{2,1,0:T(8,128)(2,1)} %o_hbm.1), custom_call_target="tpu_custom_call" | custom-call | tf_op jit(solution)/shard_map/pallas_call | solution.py:395
  98.9 1.9 %copy.8 = bf16[64,4096]{1,0:T(8,128)(2,1)} copy(bf16[64,4096]{1,0:T(8,128)(2,1)} %shard_map.64) | data formatting | bytes 1048576
